TPU v7x, 32 devices: a whole 2x2x4 slice. The times are simulated.
32 devices in a mesh: dp: 8 (over y, x, core), concept: 4 (over z).
Axes of the slice: x: 2, y: 2, z: 4, core: 2. Of those that a mesh axis runs over, the one named last changes fastest.
Arguments:
- text: bfloat16 [4096, 1024], P('dp', 'concept'), may hold values from -6 to 6
- concept_table: bfloat16 [24576, 1024], P('dp', 'concept'), may hold values from -6 to 6
- ids: int32 [4096], P('dp'), may hold values from 0 to 24575, as said below
Outputs:
- balanced: float32 [4096], P('dp')
Inputs may be any that keep to these rules, and one draw needn't show every extreme that they name: In the 512 pairs of one index of dp, at most 128 ids fall in any one aligned range of 3072 concepts (c * 3072 to (c + 1) * 3072 - 1); in each such block of pairs some range holds exactly 128.
All inputs are finite; a program needn't handle non-finite values.
Results may differ from a plain program's by a relative error of at most 0.0003.
Values may be sent and summed in bfloat16 or wider, within the bound.
No kernel may reach another device: no remote copies, remote signals or barrier semaphores. Data moves between devices by JAX's collectives and lax.ppermute only.
A program may use at most 64 MiB of HBM per device.

v0:
```python
import jax
import jax.numpy as jnp
from jax import lax
from jax.sharding import PartitionSpec as P

CAP = 16


logit_scale = 64.0
epsilon = 1e-06


def block_size(count):
    return min(512, count)


def fetch(table, wanted):
    total = wanted.shape[0]
    valid = (wanted >= 0).astype(jnp.float32)
    width = block_size(total)
    columns = jnp.arange(table.shape[0], dtype=jnp.int32)

    def one_block(block_ids):
        selector = (block_ids[:, None] == columns[None, :]).astype(jnp.bfloat16)
        return jnp.dot(selector, table, preferred_element_type=jnp.float32)

    pieces = lax.map(one_block, wanted.reshape(total // width, width)).reshape(
        total, table.shape[1]
    )
    return pieces * valid[:, None]


def tally(wanted, weights, held):
    total = wanted.shape[0]
    capped = CAP * 1.0
    width = block_size(total)
    columns = jnp.arange(held, dtype=jnp.int32)
    id_blocks = wanted.reshape(total // width, width)
    weight_blocks = weights.reshape(total // width, width)

    def add_block(args):
        block_ids, block_weights = args
        selector = (block_ids[:, None] == columns[None, :]).astype(jnp.float32)
        return jnp.dot(block_weights, selector, precision=lax.Precision.HIGHEST)

    count = jnp.sum(lax.map(add_block, (id_blocks, weight_blocks)), axis=0)

    def read_block(block_ids):
        selector = (block_ids[:, None] == columns[None, :]).astype(jnp.float32)
        return jnp.dot(selector, count, precision=lax.Precision.HIGHEST)

    looked = lax.map(read_block, id_blocks).reshape(total)
    return capped / jnp.maximum(looked, capped)


def similarity(dot, tsq, csq):
    return jax.nn.sigmoid(logit_scale * dot * lax.rsqrt(tsq + epsilon) * lax.rsqrt(csq + epsilon))


def body(text, concept_table, ids):
    groups = lax.axis_size("dp")
    pairs = text.shape[0]
    quarter = text.shape[1]
    held = concept_table.shape[0]
    slots = 2 * pairs // groups
    total = groups * slots
    owner = ids // held
    local = ids % held
    marks = (owner[:, None] == jnp.arange(groups, dtype=jnp.int32)[None, :]).astype(jnp.int32)
    ranks = jnp.sum((jnp.cumsum(marks, axis=0) - 1) * marks, axis=1)
    target = owner * slots + ranks
    slot_ids = jnp.full((total,), -1, jnp.int32).at[target].set(local)
    wanted = lax.all_to_all(
        slot_ids.reshape(groups, slots), "dp", split_axis=0, concat_axis=0, tiled=True
    ).reshape(total)
    valid = (wanted >= 0).astype(jnp.float32)
    slot_text = jnp.zeros((total, quarter), jnp.bfloat16).at[target].set(text)
    arrived = lax.all_to_all(
        slot_text.reshape(groups, slots, quarter), "dp", split_axis=0, concat_axis=0, tiled=True
    ).reshape(total, quarter)
    pieces = fetch(concept_table, wanted)
    floats = arrived.astype(jnp.float32)
    dot, tsq, csq = lax.psum(
        (
            jnp.sum(floats * pieces, axis=1),
            jnp.sum(floats * floats, axis=1),
            jnp.sum(pieces * pieces, axis=1),
        ),
        "concept",
    )
    match = similarity(dot, tsq, csq) * valid
    share = tally(wanted, match, held)
    returned = lax.all_to_all(
        (match * share).reshape(groups, slots), "dp", split_axis=0, concat_axis=0, tiled=True
    ).reshape(total)
    return jnp.take(returned, target)


def solution(mesh):
    placed = (P("dp", "concept"), P("dp", "concept"), P("dp"))
    return jax.shard_map(body, mesh=mesh, in_specs=placed, out_specs=P("dp"), check_vma=False)
```

profile of v0, /device:TPU:0, one launch (start us, length us, event | category | flops | bytes accessed | tf_op | source)
XLA Modules:
  0.0 69.9 jit_solution(9062257080505250184)
XLA Ops:
  0.0 0.8 %add_select_fusion = (s32[512]{0:T(512)S(1)}, s32[512]{0:T(512)S(1)}) fusion(s32[512]{0:T(512)} %param.11), kind=kLoop, calls=%fused_computation.42 | loop fusion | flops 6144 | bytes 6144 | tf_op jit(solution)/shard_map/jit(remainder)/select_n | solution.py:68
  0.8 1.1 %reduce-window.6 = s32[8,4,128]{2,0,1:T(8,128)S(1)} reduce-window(s32[8,4,128]{2,0,1:T(8,128)S(1)} %fusion.22, s32[]{:T(128)} %constant.56.clone.1), window={size=1x1x128 pad=0_0x0_0x127_0}, to_apply=%region_0.1 | reduce-window | flops 520192 | bytes 32772 | tf_op jit(solution)/shard_map/reduce-window
  2.3 3.0 %scatter_custom_fusion = s32[1024]{0:T(1024)} fusion(s32[512]{0:T(512)S(1)} %compare_select_fusion, s32[512]{0:T(512)S(1)} %get-tuple-element.150, s32[]{:T(128)} %constant.80.clone.1), kind=kCustom, calls=%fused_computation.45 | custom fusion | bytes 4100 | tf_op jit(solution)/shard_map/scatter | solution.py:72
  5.4 5.2 %all-to-all-start = ((s32[8,1,128]{2,1,0:T(1,128)}), s32[8,1,128]{2,1,0:T(1,128)S(1)}, u32[]{:S(2)}, u32[]{:S(2)}) async-start(s32[8,1,128]{2,1,0:T(1,128)} %bitcast.3), calls=%async_computation | async-start | bytes 8192 | tf_op jit(solution)/shard_map/all_to_all | solution.py:73
  10.6 3.5 %scatter_custom_fusion.1 = bf16[1024,256]{1,0:T(8,128)(2,1)} fusion(s32[512]{0:T(512)S(1)} %compare_select_fusion, bf16[512,256]{1,0:T(8,128)(2,1)} %param.9, bf16[]{:T(256)} %constant.85.clone.1), kind=kCustom, calls=%fused_computation.28 | custom fusion | bytes 524800 | tf_op jit(solution)/shard_map/scatter | solution.py:77
  14.1 1.1 %all-to-all-done = s32[8,1,128]{2,1,0:T(1,128)S(1)} async-done(((s32[8,1,128]{2,1,0:T(1,128)}), s32[8,1,128]{2,1,0:T(1,128)S(1)}, u32[]{:S(2)}, u32[]{:S(2)}) %all-to-all-start) | async-done | bytes 4128 | tf_op jit(solution)/shard_map/all_to_all | solution.py:73
  15.2 3.5 %all-to-all-start.1 = ((bf16[8,128,256]{2,1,0:T(8,128)(2,1)}), bf16[8,128,256]{2,1,0:T(8,128)(2,1)S(1)}, u32[]{:S(2)}, u32[]{:S(2)}) async-start(bf16[8,128,256]{2,1,0:T(8,128)(2,1)} %bitcast.6), calls=%async_computation.1 | async-start | bytes 1048576 | tf_op jit(solution)/shard_map/all_to_all | solution.py:78
  18.7 0.6 broadcast.96
  19.3 0.7 %reduce.8 = s32[8,128]{1,0:T(8,128)S(1)} reduce(s32[8,1,128]{2,1,0:T(1,128)S(1)} %all-to-all-done, s32[]{:T(128)} %broadcast.96), dimensions={1}, to_apply=%all_to_all.16.reduce_sub_computation.3 | reduce | bytes 8196 | tf_op jit(solution)/shard_map/all_to_all | solution.py:73
  20.1 2.5 %while.33 = (s32[]{:T(128)}, f32[2,512,256]{2,1,0:T(8,128)S(1)}, s32[2,512]{1,0:T(2,128)S(1)}, bf16[3072,256]{1,0:T(8,128)(2,1)S(1)}, s32[]{:T(128)}) while((s32[]{:T(128)}, f32[2,512,256]{2,1,0:T(8,128)S(1)}, s32[2,512]{1,0:T(2,128)S(1)}, bf16[3072,256]{1,0:T(8,128)(2,1)S(1)}, s32[]{:T(128)}) %tuple.67), condition=%wide.region_6.7_spmd.clone, body=%wide.region_5.6_spmd.clone.sunk | while | flops 806879232 | bytes 2103365 | solution.py:27
  20.1 1.2 %fusion.35 = f32[2,512,256]{2,1,0:T(8,128)S(1)} fusion(f32[2,512,256]{2,1,0:T(8,128)S(1)} %get-tuple-element.233, s32[]{:T(128)} %get-tuple-element.232, bf16[3072,256]{1,0:T(8,128)(2,1)S(1)} %get-tuple-element.240, s32[512]{0:T(512)S(1)} %bitcast.58), kind=kOutput, calls=%fused_computation.10.clone.1 | convolution fusion | flops 806879232 | bytes 2099204 | tf_op jit(solution)/shard_map/while/body/eval_jaxpr/dot_general | solution.py:25
  21.3 1.2 %fusion.35 = f32[2,512,256]{2,1,0:T(8,128)S(1)} fusion(f32[2,512,256]{2,1,0:T(8,128)S(1)} %get-tuple-element.233, s32[]{:T(128)} %get-tuple-element.232, bf16[3072,256]{1,0:T(8,128)(2,1)S(1)} %get-tuple-element.240, s32[512]{0:T(512)S(1)} %bitcast.58), kind=kOutput, calls=%fused_computation.10.clone.1 | convolution fusion | flops 806879232 | bytes 2099204 | tf_op jit(solution)/shard_map/while/body/eval_jaxpr/dot_general | solution.py:25
  23.0 5.4 %all-to-all-done.1 = bf16[8,128,256]{2,1,0:T(8,128)(2,1)S(1)} async-done(((bf16[8,128,256]{2,1,0:T(8,128)(2,1)}), bf16[8,128,256]{2,1,0:T(8,128)(2,1)S(1)}, u32[]{:S(2)}, u32[]{:S(2)}) %all-to-all-start.1) | async-done | bytes 524320 | tf_op jit(solution)/shard_map/all_to_all | solution.py:78
  28.9 18.9 %all-reduce = (f32[1024]{0:T(1024)S(1)}, f32[1024]{0:T(1024)S(1)}, f32[1024]{0:T(1024)S(1)}) all-reduce(f32[1024]{0:T(1024)S(1)} %bitcast.66, f32[1024]{0:T(1024)S(1)} %bitcast.64, f32[1024]{0:T(1024)S(1)} %bitcast.63), channel_id=1, replica_groups=mesh['dp'=8,'concept'=4] {'concept'}, use_global_device_ids=true, to_apply=%region_12.13 | all-reduce | flops 3072 | bytes 24576 | tf_op jit(solution)/shard_map/psum | solution.py:83
  47.9 4.5 %while.34 = (s32[]{:T(128)}, f32[2,3072]{1,0:T(2,128)S(1)}, f32[2,512]{1,0:T(2,128)S(1)}, s32[2,512]{1,0:T(2,128)S(1)}, s32[]{:T(128)}, /*index=5*/s32[]{:T(128)}) while((s32[]{:T(128)}, f32[2,3072]{1,0:T(2,128)S(1)}, f32[2,512]{1,0:T(2,128)S(1)}, s32[2,512]{1,0:T(2,128)S(1)}, s32[]{:T(128)}, /*index=5*/s32[]{:T(128)}) %tuple.65), condition=%wide.region_14.15_spmd.clone, body=%wide.region_13.14_spmd.clone.sunk | while | flops 20447232 | bytes 45137 | solution.py:46
  47.9 2.1 %fusion.37 = f32[1,3072]{1,0:T(1,128)S(1)} fusion(s32[512]{0:T(512)S(1)} %bitcast.59, f32[2,512]{1,0:T(2,128)S(1)} %get-tuple-element.256, s32[]{:T(128)} %get-tuple-element.248), kind=kOutput, calls=%fused_computation.13.clone.1 | convolution fusion | flops 20447232 | bytes 16388 | tf_op jit(solution)/shard_map/while/body/eval_jaxpr/dot_general | solution.py:44
  50.2 2.1 %fusion.37 = f32[1,3072]{1,0:T(1,128)S(1)} fusion(s32[512]{0:T(512)S(1)} %bitcast.59, f32[2,512]{1,0:T(2,128)S(1)} %get-tuple-element.256, s32[]{:T(128)} %get-tuple-element.248), kind=kOutput, calls=%fused_computation.13.clone.1 | convolution fusion | flops 20447232 | bytes 16388 | tf_op jit(solution)/shard_map/while/body/eval_jaxpr/dot_general | solution.py:44
  52.4 6.0 %while.35 = (s32[]{:T(128)}, f32[2,512]{1,0:T(2,128)S(1)}, s32[2,512]{1,0:T(2,128)S(1)}, f32[3072]{0:T(1024)S(1)}, s32[]{:T(128)}, /*index=5*/s32[]{:T(128)}) while((s32[]{:T(128)}, f32[2,512]{1,0:T(2,128)S(1)}, s32[2,512]{1,0:T(2,128)S(1)}, f32[3072]{0:T(1024)S(1)}, s32[]{:T(128)}, /*index=5*/s32[]{:T(128)}) %tuple.66), condition=%wide.region_17.18_spmd.clone, body=%wide.region_16.17_spmd.clone.sunk | while | flops 20447232 | bytes 24653 | solution.py:52
  52.5 2.9 %fusion.39 = f32[1,512]{1,0:T(1,128)S(1)} fusion(f32[3072,1]{0,1:T(1,128)S(1)} %bitcast.68, s32[512]{0:T(512)S(1)} %bitcast.60), kind=kOutput, calls=%fused_computation.20.clone.1 | convolution fusion | flops 20447232 | bytes 16384 | tf_op jit(solution)/shard_map/while/body/eval_jaxpr/dot_general | solution.py:50
  55.5 2.9 %fusion.39 = f32[1,512]{1,0:T(1,128)S(1)} fusion(f32[3072,1]{0,1:T(1,128)S(1)} %bitcast.68, s32[512]{0:T(512)S(1)} %bitcast.60), kind=kOutput, calls=%fused_computation.20.clone.1 | convolution fusion | flops 20447232 | bytes 16384 | tf_op jit(solution)/shard_map/while/body/eval_jaxpr/dot_general | solution.py:50
  58.5 0.6 mul.68
  59.1 3.3 %all-to-all-start.2 = ((f32[8,1,128]{2,1,0:T(1,128)}), f32[8,1,128]{2,1,0:T(1,128)S(1)}, u32[]{:S(2)}, u32[]{:S(2)}) async-start(f32[8,1,128]{2,1,0:T(1,128)} %bitcast.11), calls=%async_computation.2 | async-start | bytes 8192 | tf_op jit(solution)/shard_map/all_to_all | solution.py:93
  62.4 4.6 %all-to-all-done.2 = f32[8,1,128]{2,1,0:T(1,128)S(1)} async-done(((f32[8,1,128]{2,1,0:T(1,128)}), f32[8,1,128]{2,1,0:T(1,128)S(1)}, u32[]{:S(2)}, u32[]{:S(2)}) %all-to-all-start.2) | async-done | bytes 4128 | tf_op jit(solution)/shard_map/all_to_all | solution.py:93
  67.0 2.3 %gather_fusion = f32[512]{0:T(512)S(1)} fusion(f32[1024]{0:T(1024)S(1)} %bitcast.56, s32[1024]{0:T(1024)S(1)} %pad_clamp_fusion), kind=kCustom, calls=%fused_computation | custom fusion | bytes 6144 | tf_op jit(solution)/shard_map/jit(_take)/gather | solution.py:96
  (34 shorter events, 2.3 us)
Async XLA Ops:
  0.0 20.1 %copy-start = (bf16[3072,256]{1,0:T(8,128)(2,1)S(1)}, bf16[3072,256]{1,0:T(8,128)(2,1)}, u32[]{:S(2)}) copy-start(bf16[3072,256]{1,0:T(8,128)(2,1)} %param.10) | copy-start | bytes 4718596
  5.4 9.9 %all-to-all-start = ((s32[8,1,128]{2,1,0:T(1,128)}), s32[8,1,128]{2,1,0:T(1,128)S(1)}, u32[]{:S(2)}, u32[]{:S(2)}) async-start(s32[8,1,128]{2,1,0:T(1,128)} %bitcast.3), calls=%async_computation | async-start | bytes 8192 | tf_op jit(solution)/shard_map/all_to_all | solution.py:73
  15.2 13.1 %all-to-all-start.1 = ((bf16[8,128,256]{2,1,0:T(8,128)(2,1)}), bf16[8,128,256]{2,1,0:T(8,128)(2,1)S(1)}, u32[]{:S(2)}, u32[]{:S(2)}) async-start(bf16[8,128,256]{2,1,0:T(8,128)(2,1)} %bitcast.6), calls=%async_computation.1 | async-start | bytes 1048576 | tf_op jit(solution)/shard_map/all_to_all | solution.py:78
  59.1 8.0 %all-to-all-start.2 = ((f32[8,1,128]{2,1,0:T(1,128)}), f32[8,1,128]{2,1,0:T(1,128)S(1)}, u32[]{:S(2)}, u32[]{:S(2)}) async-start(f32[8,1,128]{2,1,0:T(1,128)} %bitcast.11), calls=%async_computation.2 | async-start | bytes 8192 | tf_op jit(solution)/shard_map/all_to_all | solution.py:93
where the time goes:
time: 70.3 us; the launch traced here: 69.9 us
  blocking collectives  18.9 us (27%)
  matrix products  12.5 us (18%)
  starting transfers between devices  12 us (17%)
  waiting for transfers between devices  11.2 us (16%)
  local copies, waits for them, and re-layouts  10 us (14%)
  other arithmetic  4.94 us (7%)
    psum x1, blocking collectives, body(): lax.psum((jnp.sum(floats * pieces, axis=1), jnp.sum(floats * floats, axis...  18.9 us
    dot_general x2, matrix products, read_block(): return jnp.dot(selector, count, precision=lax.Precision.HIGHEST)  5.86 us
    all_to_all x1, waiting for transfers between devices, body(): lax.all_to_all(slot_text.reshape(groups, slots, quarter), 'dp', split_axi...  5.43 us
    all_to_all x1, starting transfers between devices, body(): lax.all_to_all(slot_ids.reshape(groups, slots), 'dp', split_axis=0, conca...  5.2 us
    all_to_all x1, waiting for transfers between devices, body(): lax.all_to_all((match * share).reshape(groups, slots), 'dp', split_axis=0...  4.6 us
    dot_general x2, matrix products, add_block(): return jnp.dot(block_weights, selector, precision=lax.Precision.HIGHEST)  4.23 us
    scatter x1, local copies, waits for them, and re-layouts, body(): slot_text = jnp.zeros((total, quarter), jnp.bfloat16).at[target].set(text)  3.53 us
    all_to_all x1, starting transfers between devices, body(): lax.all_to_all(slot_text.reshape(groups, slots, quarter), 'dp', split_axi...  3.49 us
  transfers between devices with their start and end apart: 3, of which 3 were waited for; matrix products, arithmetic and copies ran while one was open for 11% of the time, Pallas kernels for 0%

commit v1 on v0

v1 whole, which is shorter than its diff:
```python
import functools

import jax
import jax.numpy as jnp
from jax import lax
from jax.experimental import pallas as pl
from jax.experimental.pallas import tpu as pltpu
from jax.sharding import PartitionSpec as P

CAP = 16
BASE = 256
LANES = 128
EXTRA = 8

logit_scale = 64.0
epsilon = 1e-06

VMEM = pl.BlockSpec(memory_space=pltpu.VMEM)


def split3(values):
    first = values.astype(jnp.bfloat16)
    rest = values - first.astype(jnp.float32)
    second = rest.astype(jnp.bfloat16)
    third = (rest - second.astype(jnp.float32)).astype(jnp.bfloat16)
    return first, second, third


def contract_lanes(left, right):
    return lax.dot_general(left, right, (((1,), (1,)), ((), ())), preferred_element_type=jnp.float32)


def slot_kernel(groups, slots, held, ids_ref, text_ref, out_ref, mark_ref, rank_ref):
    ids = ids_ref[...]
    pairs = ids.shape[1]
    group = lax.broadcasted_iota(jnp.int32, (groups, pairs), 0)
    start = group * held
    marks = jnp.where((ids >= start) & (ids < start + held), 1.0, 0.0)
    before = lax.broadcasted_iota(jnp.int32, (pairs, pairs), 0) < lax.broadcasted_iota(jnp.int32, (pairs, pairs), 1)
    triangle = jnp.where(before, 1.0, 0.0).astype(jnp.bfloat16)
    seen = jnp.dot(marks.astype(jnp.bfloat16), triangle, preferred_element_type=jnp.float32)
    rank = jnp.sum(marks * seen, axis=0, keepdims=True)
    owner = jnp.sum(marks * group.astype(jnp.float32), axis=0, keepdims=True)
    local = ids.astype(jnp.float32) - owner * held
    high = jnp.floor(local * (1.0 / BASE))
    low = local - high * BASE
    target = (owner * slots + rank).astype(jnp.int32)
    places = lax.broadcasted_iota(jnp.int32, (groups * slots, pairs), 0)
    chosen = jnp.where(places == target, 1.0, 0.0).astype(jnp.bfloat16)
    row = lax.broadcasted_iota(jnp.int32, (EXTRA, pairs), 0)
    digits = jnp.where(row == 0, low, jnp.where(row == 1, high + 1.0, 0.0)).astype(jnp.bfloat16)
    features = text_ref[...].T
    moved = contract_lanes(features, chosen).astype(jnp.bfloat16)
    named = contract_lanes(digits, chosen).astype(jnp.bfloat16)
    depth = features.shape[0]
    if slots % LANES == 0:
        for g in range(groups):
            out_ref[g, :depth, :] = moved[:, g * slots : (g + 1) * slots]
            out_ref[g, depth:, :] = named[:, g * slots : (g + 1) * slots]
    else:
        out_ref[:depth, :] = moved
        out_ref[depth:, :] = named
    mark_ref[...] = marks
    rank_ref[...] = rank


def read(ref, rows, at, width):
    if len(ref.shape) == 2:
        return ref[rows, at : at + width]
    slots = ref.shape[2]
    pieces = []
    while width:
        g, offset = divmod(at, slots)
        step = min(width, slots - offset)
        pieces.append(ref[g, rows, offset : offset + step])
        at, width = at + step, width - step
    return pieces[0] if len(pieces) == 1 else jnp.concatenate(pieces, axis=1)


def match_kernel(total, depth, arrived_ref, table_ref, part_ref, digit_ref):
    blocks = table_ref.shape[0]
    width = 2 * LANES if total % (2 * LANES) == 0 else LANES
    half = depth // 2 if depth % 32 == 0 else depth
    low_of = lax.broadcasted_iota(jnp.int32, (BASE, width), 0).astype(jnp.float32)
    for at in range(0, total, width):
        digits = read(arrived_ref, slice(depth, depth + EXTRA), at, width).astype(jnp.float32)
        low, high = digits[0:1], digits[1:2]
        lows = jnp.where(low_of == low, 1.0, 0.0).astype(jnp.bfloat16)
        dot = tsq = csq = jnp.zeros((1, width), jnp.float32)
        for top in range(0, depth, half):
            pieces = jnp.zeros((half, width), jnp.float32)
            for block in range(blocks):
                found = jnp.dot(table_ref[block, top : top + half, :], lows, preferred_element_type=jnp.float32)
                pieces = jnp.where(high == block + 1.0, found, pieces)
            floats = read(arrived_ref, slice(top, top + half), at, width).astype(jnp.float32)
            dot += jnp.sum(floats * pieces, axis=0, keepdims=True)
            tsq += jnp.sum(floats * floats, axis=0, keepdims=True)
            csq += jnp.sum(pieces * pieces, axis=0, keepdims=True)
        for step in range(width // LANES):
            lane = slice(step * LANES, (step + 1) * LANES)
            b = at // LANES + step
            for q, sums in enumerate((dot, tsq, csq)):
                part_ref[q, b : b + 1, :] = sums[:, lane]
            digit_ref[0, b : b + 1, :] = low[:, lane]
            digit_ref[1, b : b + 1, :] = high[:, lane]


def count_kernel(highs, *refs):
    *part_refs, digit_ref, out_ref = refs
    sums = [ref[...] for ref in part_refs]
    while len(sums) > 1:
        sums = [sums[i] + sums[i + 1] for i in range(0, len(sums), 2)]
    dot, tsq, csq = sums[0][0], sums[0][1], sums[0][2]
    match = jax.nn.sigmoid(logit_scale * dot * lax.rsqrt(tsq + epsilon) * lax.rsqrt(csq + epsilon))
    capped = CAP * 1.0
    blocks = match.shape[0]
    line = lambda rows: jnp.concatenate([rows[b : b + 1] for b in range(blocks)], axis=1)
    weights, low, high = line(match), line(digit_ref[0]), line(digit_ref[1])
    total = weights.shape[1]
    lows = jnp.where(lax.broadcasted_iota(jnp.int32, (BASE, total), 0).astype(jnp.float32) == low, 1.0, 0.0).astype(jnp.bfloat16)
    tops = jnp.where(lax.broadcasted_iota(jnp.int32, (highs, total), 0).astype(jnp.float32) + 1.0 == high, 1.0, 0.0)
    spread = jnp.concatenate(split3(tops * weights), axis=0)
    parts = contract_lanes(spread, lows)
    count = parts[:highs] + parts[highs : 2 * highs] + parts[2 * highs :]
    parts = jnp.dot(jnp.concatenate(split3(count), axis=0), lows, preferred_element_type=jnp.float32)
    looked = jnp.sum(tops * (parts[:highs] + parts[highs : 2 * highs] + parts[2 * highs :]), axis=0, keepdims=True)
    balanced = weights * capped / jnp.maximum(looked, capped)
    for b in range(blocks):
        out_ref[b : b + 1, :] = balanced[:, b * LANES : (b + 1) * LANES]


def unslot_kernel(returned_ref, mark_ref, rank_ref, out_ref):
    groups, slots = returned_ref.shape
    pairs = mark_ref.shape[1]
    ranks = lax.broadcasted_iota(jnp.int32, (slots, pairs), 0).astype(jnp.float32)
    chosen = jnp.where(ranks == rank_ref[...], 1.0, 0.0).astype(jnp.bfloat16)
    first, second, third = (jnp.dot(part, chosen, preferred_element_type=jnp.float32) for part in split3(returned_ref[...]))
    out_ref[...] = jnp.sum(mark_ref[...] * (first + second + third), axis=0, keepdims=True)


def body(text, concept_table, ids):
    groups = lax.axis_size("dp")
    quarters = lax.axis_size("concept")
    pairs, depth = text.shape
    held = concept_table.shape[0]
    slots = 2 * pairs // groups
    total = groups * slots
    f32 = jnp.float32
    blocks = -(-held // BASE)
    wide = slots % LANES == 0
    sent_shape = (groups, depth + EXTRA, slots) if wide else (depth + EXTRA, total)

    sent, marks, rank = pl.pallas_call(
        functools.partial(slot_kernel, groups, slots, held),
        out_shape=(
            jax.ShapeDtypeStruct(sent_shape, jnp.bfloat16),
            jax.ShapeDtypeStruct((groups, pairs), f32),
            jax.ShapeDtypeStruct((1, pairs), f32),
        ),
        in_specs=[VMEM] * 2,
        out_specs=(VMEM,) * 3,
        name="slot",
    )(ids.reshape(1, pairs), text)
    if not wide:
        sent = sent.reshape(depth + EXTRA, groups, slots).transpose(1, 0, 2)
    arrived = lax.all_to_all(sent, "dp", split_axis=0, concat_axis=0, tiled=True)
    if not wide:
        arrived = arrived.transpose(1, 0, 2).reshape(depth + EXTRA, total)

    padded = jnp.pad(concept_table, ((0, blocks * BASE - held), (0, 0)))
    turned = padded.reshape(blocks, BASE, depth).transpose(0, 2, 1)

    part, digits = pl.pallas_call(
        functools.partial(match_kernel, total, depth),
        out_shape=(
            jax.ShapeDtypeStruct((3, total // LANES, LANES), f32),
            jax.ShapeDtypeStruct((2, total // LANES, LANES), f32),
        ),
        in_specs=[VMEM] * 2,
        out_specs=(VMEM,) * 2,
        name="match",
    )(arrived, turned)

    if quarters & (quarters - 1) == 0:
        parts = [part] + [
            lax.ppermute(part, "concept", [(i, i ^ step) for i in range(quarters)]) for step in range(1, quarters)
        ]
    else:
        parts = [lax.psum(part, "concept")]

    balanced = pl.pallas_call(
        functools.partial(count_kernel, -(-blocks // 16) * 16),
        out_shape=jax.ShapeDtypeStruct((total // LANES, LANES), f32),
        in_specs=[VMEM] * (len(parts) + 1),
        out_specs=VMEM,
        name="count",
    )(*parts, digits)

    returned = lax.all_to_all(balanced.reshape(groups, slots), "dp", split_axis=0, concat_axis=0, tiled=True)

    out = pl.pallas_call(
        unslot_kernel,
        out_shape=jax.ShapeDtypeStruct((1, pairs), f32),
        in_specs=[VMEM] * 3,
        out_specs=VMEM,
        name="unslot",
    )(returned, marks, rank)
    return out.reshape(pairs)


def solution(mesh):
    placed = (P("dp", "concept"), P("dp", "concept"), P("dp"))
    return jax.shard_map(body, mesh=mesh, in_specs=placed, out_specs=P("dp"), check_vma=False)
```

time: 70.3 us -> 44 us (0.63)
  matrix products: 12.5 us -> 0 us
  blocking collectives: 18.9 us -> 8.49 us
  Pallas kernels: 0 us -> 10.2 us
  local copies, waits for them, and re-layouts: 10 us -> 4.01 us
  other arithmetic: 4.94 us -> 0 us
  starting transfers between devices: 12 us -> 9.59 us
    psum x1 -> x0, blocking collectives: 18.9 us -> none  [body(): lax.psum((jnp.sum(floats * pieces, axis=1), jnp.sum(floats * floats, axis...]
    dot_general x6 -> x0, matrix products: 12.5 us -> none  [the longest x2 5.86 us: read_block(): return jnp.dot(selector, count, precision=lax.Precision.HIGHEST)]
    pallas_call x0 -> x4, Pallas kernels: none -> 10.2 us  [the longest x1 4.04 us: body(): pl.pallas_call(functools.partial(match_kernel, total, depth), out_shape=(...]
    all_to_all x0 -> x1, blocking collectives: none -> 8.49 us  [body(): lax.all_to_all(balanced.reshape(groups, slots), 'dp', split_axis=0, conca...]
    all_to_all x3 -> x1, starting transfers between devices: 12 us -> 5.2 us  [body(): lax.all_to_all(sent, 'dp', split_axis=0, concat_axis=0, tiled=True)]
    scatter x2 -> x0, local copies, waits for them, and re-layouts: 6.54 us -> none  [the longest x1 3.53 us: body(): slot_text = jnp.zeros((total, quarter), jnp.bfloat16).at[target].set(text)]
    ppermute x0 -> x3, starting transfers between devices: none -> 4.39 us  [body(): lax.ppermute(part, 'concept', [(i, i ^ step) for i in range(quarters)])]
    ppermute x0 -> x3, waiting for transfers between devices: none -> 4.03 us  [body(): lax.ppermute(part, 'concept', [(i, i ^ step) for i in range(quarters)])]
  transfers between devices with their start and end apart: 3 -> 4, of which waited for: 3 -> 3; matrix products, arithmetic and copies ran while one was open for 11% -> 6% of each run, Pallas kernels for 0% -> 0%
where the time goes in v1:
time: 44 us; the launch traced here: 43.6 us
  waiting for transfers between devices  11.3 us (26%)
  Pallas kernels  10.2 us (23%)
  starting transfers between devices  9.59 us (22%)
  blocking collectives  8.49 us (19%)
  local copies, waits for them, and re-layouts  4.01 us (9%)
    all_to_all x1, blocking collectives, body(): lax.all_to_all(balanced.reshape(groups, slots), 'dp', split_axis=0, conca...  8.49 us
    all_to_all x1, waiting for transfers between devices, body(): lax.all_to_all(sent, 'dp', split_axis=0, concat_axis=0, tiled=True)  7.27 us
    all_to_all x1, starting transfers between devices, body(): lax.all_to_all(sent, 'dp', split_axis=0, concat_axis=0, tiled=True)  5.2 us
    ppermute x3, starting transfers between devices, body(): lax.ppermute(part, 'concept', [(i, i ^ step) for i in range(quarters)])  4.39 us
    pallas_call x1, Pallas kernels, body(): pl.pallas_call(functools.partial(match_kernel, total, depth), out_shape=(...  4.04 us
    ppermute x3, waiting for transfers between devices, body(): lax.ppermute(part, 'concept', [(i, i ^ step) for i in range(quarters)])  4.03 us
    pallas_call x1, Pallas kernels, body(): pl.pallas_call(functools.partial(slot_kernel, groups, slots, held), out_s...  2.7 us
    reshape x1, local copies, waits for them, and re-layouts, body(): turned = padded.reshape(blocks, BASE, depth).transpose(0, 2, 1)  2.61 us
  transfers between devices with their start and end apart: 4, of which 3 were waited for; matrix products, arithmetic and copies ran while one was open for 6% of the time, Pallas kernels for 0%

profile of v1, /device:TPU:0, one launch (start us, length us, event | category | flops | bytes accessed | tf_op | source)
XLA Modules:
  0.0 43.6 jit_solution(7930206741055215603)
XLA Ops:
  0.0 2.7 %slot.1 = (bf16[8,264,128]{2,1,0:T(8,128)(2,1)}, f32[8,512]{1,0:T(8,128)}, f32[1,512]{1,0:T(1,128)}) custom-call(s32[1,512]{1,0:T(1,128)} %bitcast.12, bf16[512,256]{1,0:T(8,128)(2,1)} %text_ref.1), custom_call_target="tpu_custom_call" | custom-call | tf_op jit(solution)/shard_map/slot/pallas_call | solution.py:153
  2.7 5.2 %all-to-all-start = ((bf16[8,264,128]{2,1,0:T(8,128)(2,1)}), bf16[8,264,128]{2,1,0:T(8,128)(2,1)S(1)}, u32[]{:S(2)}, u32[]{:S(2)}) async-start(bf16[8,264,128]{2,1,0:T(8,128)(2,1)} %get-tuple-element.10), calls=%async_computation | async-start | bytes 1081344 | tf_op jit(solution)/shard_map/all_to_all | solution.py:166
  7.9 2.6 %copy.5 = bf16[12,256,256]{1,2,0:T(8,128)(2,1)} copy(bf16[12,256,256]{2,1,0:T(8,128)(2,1)} %bitcast.9) | data formatting | bytes 3145728 | tf_op jit(solution)/shard_map/reshape | solution.py:171
  10.5 7.3 %all-to-all-done.arrived_ref = bf16[8,264,128]{2,1,0:T(8,128)(2,1)S(1)} async-done(((bf16[8,264,128]{2,1,0:T(8,128)(2,1)}), bf16[8,264,128]{2,1,0:T(8,128)(2,1)S(1)}, u32[]{:S(2)}, u32[]{:S(2)}) %all-to-all-start) | async-done | bytes 540704 | tf_op jit(solution)/shard_map/all_to_all | solution.py:166
  17.8 0.0 copy-start
  17.8 0.8 %copy-done = bf16[8,264,128]{2,1,0:T(8,128)(2,1)} copy-done((bf16[8,264,128]{2,1,0:T(8,128)(2,1)}, bf16[8,264,128]{2,1,0:T(8,128)(2,1)S(1)}, u32[]{:S(2)}) %copy-start) | copy-done | bytes 540696
  18.6 4.0 %match.1 = (f32[3,8,128]{2,1,0:T(8,128)}, f32[2,8,128]{2,1,0:T(8,128)}) custom-call(bf16[8,264,128]{2,1,0:T(8,128)(2,1)} %copy-done, bf16[12,256,256]{2,1,0:T(8,128)(2,1)} %bitcast.8), custom_call_target="tpu_custom_call" | custom-call | tf_op jit(solution)/shard_map/match/pallas_call | solution.py:173
  22.6 3.6 %collective-permute-start.2 = (f32[3,8,128]{2,1,0:T(8,128)}, f32[3,8,128]{2,1,0:T(8,128)S(1)}, u32[]{:S(2)}, u32[]{:S(2)}) collective-permute-start(f32[3,8,128]{2,1,0:T(8,128)} %get-tuple-element.11.refs_0_), channel_id=1, source_target_pairs={{0,3},{1,2},{2,1},{3,0},{4,7},{5,6},{6,5},{7,4},{8,11},{9,10},{10,... | collective-permute-start | bytes 36872 | tf_op jit(solution)/shard_map/ppermute | solution.py:186
  26.2 0.0 collective-permute-start.1
  26.2 0.8 %collective-permute-start = (f32[3,8,128]{2,1,0:T(8,128)}, f32[3,8,128]{2,1,0:T(8,128)S(1)}, u32[]{:S(2)}, u32[]{:S(2)}) collective-permute-start(f32[3,8,128]{2,1,0:T(8,128)} %get-tuple-element.11.refs_0_), channel_id=1, source_target_pairs={{0,1},{1,0},{2,3},{3,2},{4,5},{5,4},{6,7},{7,6},{8,9},{9,8},{10,11... | collective-permute-start | bytes 36872 | tf_op jit(solution)/shard_map/ppermute | solution.py:186
  27.0 1.3 %collective-permute-done.2.refs_3_ = f32[3,8,128]{2,1,0:T(8,128)S(1)} collective-permute-done((f32[3,8,128]{2,1,0:T(8,128)}, f32[3,8,128]{2,1,0:T(8,128)S(1)}, u32[]{:S(2)}, u32[]{:S(2)}) %collective-permute-start.2) | collective-permute-done | bytes 12320 | tf_op jit(solution)/shard_map/ppermute | solution.py:186
  28.3 0.0 copy-start.1
  28.3 2.7 %collective-permute-done.1.refs_2_ = f32[3,8,128]{2,1,0:T(8,128)S(1)} collective-permute-done((f32[3,8,128]{2,1,0:T(8,128)}, f32[3,8,128]{2,1,0:T(8,128)S(1)}, u32[]{:S(2)}, u32[]{:S(2)}) %collective-permute-start.1) | collective-permute-done | bytes 12320 | tf_op jit(solution)/shard_map/ppermute | solution.py:186
  31.0 0.0 copy-start.2
  31.0 0.0 collective-permute-done.refs_1_
  31.1 0.0 copy-start.3
  31.1 0.0 copy-done.1
  31.1 0.6 %copy-done.2 = f32[3,8,128]{2,1,0:T(8,128)} copy-done((f32[3,8,128]{2,1,0:T(8,128)}, f32[3,8,128]{2,1,0:T(8,128)S(1)}, u32[]{:S(2)}) %copy-start.2) | copy-done | bytes 12312
  31.6 0.0 copy-done.3
  31.7 1.9 %count.1 = f32[8,128]{1,0:T(8,128)} custom-call(f32[3,8,128]{2,1,0:T(8,128)} %get-tuple-element.11.refs_0_, f32[3,8,128]{2,1,0:T(8,128)} %copy-done.3, f32[3,8,128]{2,1,0:T(8,128)} %copy-done.2, f32[3,8,128]{2,1,0:T(8,128)} %copy-done.1, f32[2,8,128]{2,1,0:T(8,128)} %get-tuple-element.12.refs_4_), custom_call_target="tpu_custom_call" | custom-call | tf_op jit(solution)/shard_map/count/pallas_call | solution.py:191
  33.6 8.5 %all_to_all.16 = f32[8,1,128]{2,1,0:T(1,128)} all-to-all(f32[8,1,128]{2,1,0:T(1,128)} %bitcast.11), channel_id=1, replica_groups=mesh['dp'=8,'concept'=4] {'dp'}, dimensions={0} | all-to-all | bytes 8192 | tf_op jit(solution)/shard_map/all_to_all | solution.py:199
  42.1 1.5 %unslot.1 = f32[1,512]{1,0:T(1,128)} custom-call(f32[8,128]{1,0:T(8,128)} %bitcast.10, f32[8,512]{1,0:T(8,128)} %get-tuple-element.13.mark_ref, f32[1,512]{1,0:T(1,128)} %get-tuple-element.14.rank_ref), custom_call_target="tpu_custom_call" | custom-call | tf_op jit(solution)/shard_map/unslot/pallas_call | solution.py:201
Async XLA Ops:
  2.7 15.1 %all-to-all-start = ((bf16[8,264,128]{2,1,0:T(8,128)(2,1)}), bf16[8,264,128]{2,1,0:T(8,128)(2,1)S(1)}, u32[]{:S(2)}, u32[]{:S(2)}) async-start(bf16[8,264,128]{2,1,0:T(8,128)(2,1)} %get-tuple-element.10), calls=%async_computation | async-start | bytes 1081344 | tf_op jit(solution)/shard_map/all_to_all | solution.py:166
  17.8 0.8 %copy-start = (bf16[8,264,128]{2,1,0:T(8,128)(2,1)}, bf16[8,264,128]{2,1,0:T(8,128)(2,1)S(1)}, u32[]{:S(2)}) copy-start(bf16[8,264,128]{2,1,0:T(8,128)(2,1)S(1)} %all-to-all-done.arrived_ref) | copy-start | bytes 1622020
  22.6 5.7 %collective-permute-start.2 = (f32[3,8,128]{2,1,0:T(8,128)}, f32[3,8,128]{2,1,0:T(8,128)S(1)}, u32[]{:S(2)}, u32[]{:S(2)}) collective-permute-start(f32[3,8,128]{2,1,0:T(8,128)} %get-tuple-element.11.refs_0_), channel_id=1, source_target_pairs={{0,3},{1,2},{2,1},{3,0},{4,7},{5,6},{6,5},{7,4},{8,11},{9,10},{10,... | collective-permute-start | bytes 36872 | tf_op jit(solution)/shard_map/ppermute | solution.py:186
  26.2 4.8 %collective-permute-start.1 = (f32[3,8,128]{2,1,0:T(8,128)}, f32[3,8,128]{2,1,0:T(8,128)S(1)}, u32[]{:S(2)}, u32[]{:S(2)}) collective-permute-start(f32[3,8,128]{2,1,0:T(8,128)} %get-tuple-element.11.refs_0_), channel_id=1, source_target_pairs={{0,2},{1,3},{2,0},{3,1},{4,6},{5,7},{6,4},{7,5},{8,10},{9,11},{10,... | collective-permute-start | bytes 36872 | tf_op jit(solution)/shard_map/ppermute | solution.py:186
  26.2 4.8 %collective-permute-start = (f32[3,8,128]{2,1,0:T(8,128)}, f32[3,8,128]{2,1,0:T(8,128)S(1)}, u32[]{:S(2)}, u32[]{:S(2)}) collective-permute-start(f32[3,8,128]{2,1,0:T(8,128)} %get-tuple-element.11.refs_0_), channel_id=1, source_target_pairs={{0,1},{1,0},{2,3},{3,2},{4,5},{5,4},{6,7},{7,6},{8,9},{9,8},{10,11... | collective-permute-start | bytes 36872 | tf_op jit(solution)/shard_map/ppermute | solution.py:186
  28.3 2.7 %copy-start.1 = (f32[3,8,128]{2,1,0:T(8,128)}, f32[3,8,128]{2,1,0:T(8,128)S(1)}, u32[]{:S(2)}) copy-start(f32[3,8,128]{2,1,0:T(8,128)S(1)} %collective-permute-done.2.refs_3_) | copy-start | bytes 36868
  31.0 0.6 %copy-start.2 = (f32[3,8,128]{2,1,0:T(8,128)}, f32[3,8,128]{2,1,0:T(8,128)S(1)}, u32[]{:S(2)}) copy-start(f32[3,8,128]{2,1,0:T(8,128)S(1)} %collective-permute-done.1.refs_2_) | copy-start | bytes 36868
  31.1 0.6 %copy-start.3 = (f32[3,8,128]{2,1,0:T(8,128)}, f32[3,8,128]{2,1,0:T(8,128)S(1)}, u32[]{:S(2)}) copy-start(f32[3,8,128]{2,1,0:T(8,128)S(1)} %collective-permute-done.refs_1_) | copy-start | bytes 36868

commit v2 on v1

--- a/solution.py
+++ b/solution.py
@@ -16,6 +16,7 @@
 epsilon = 1e-06
 
 VMEM = pl.BlockSpec(memory_space=pltpu.VMEM)
+GRANT = pltpu.CompilerParams(vmem_limit_bytes=16 * 1024 * 1024)
 
 
 def split3(values):
@@ -178,6 +179,7 @@
         ),
         in_specs=[VMEM] * 2,
         out_specs=(VMEM,) * 2,
+        compiler_params=GRANT,
         name="match",
     )(arrived, turned)
 
@@ -193,6 +195,7 @@
         out_shape=jax.ShapeDtypeStruct((total // LANES, LANES), f32),
         in_specs=[VMEM] * (len(parts) + 1),
         out_specs=VMEM,
+        compiler_params=GRANT,
         name="count",
     )(*parts, digits)
 
@@ -203,6 +206,7 @@
         out_shape=jax.ShapeDtypeStruct((1, pairs), f32),
         in_specs=[VMEM] * 3,
         out_specs=VMEM,
+        compiler_params=GRANT,
         name="unslot",
     )(returned, marks, rank)
     return out.reshape(pairs)

time: 44 us -> 36.7 us (0.83)
  Pallas kernels: 10.2 us -> 5.98 us
  local copies, waits for them, and re-layouts: 4.01 us -> 1.71 us
  blocking collectives: 8.49 us -> 7.05 us
  waiting for transfers between devices: 11.3 us -> 11.9 us
    pallas_call x1, Pallas kernels: 4.04 us -> 1.93 us  [body(): pl.pallas_call(functools.partial(match_kernel, total, depth), out_shape=(...]
    all_to_all x1, blocking collectives: 8.49 us -> 7.05 us  [body(): lax.all_to_all(balanced.reshape(groups, slots), 'dp', split_axis=0, conca...]
    unnamed x8 -> x4, local copies, waits for them, and re-layouts: 1.4 us -> 0.01 us
    pallas_call x1, Pallas kernels: 1.94 us -> 0.58 us  [body(): pl.pallas_call(functools.partial(count_kernel, -(-blocks // 16) * 16), ou...]
    reshape x1, local copies, waits for them, and re-layouts: 2.61 us -> 1.7 us  [body(): turned = padded.reshape(blocks, BASE, depth).transpose(0, 2, 1)]
    all_to_all x1, waiting for transfers between devices: 7.27 us -> 8.16 us  [body(): lax.all_to_all(sent, 'dp', split_axis=0, concat_axis=0, tiled=True)]
    pallas_call x1, Pallas kernels: 1.48 us -> 0.76 us  [body(): pl.pallas_call(unslot_kernel, out_shape=jax.ShapeDtypeStruct((1, pairs),...]
  transfers between devices with their start and end apart: 4 -> 4, of which waited for: 3 -> 3; matrix products, arithmetic and copies ran while one was open for 6% -> 5% of each run, Pallas kernels for 0% -> 0%
where the time goes in v2:
time: 36.7 us; the launch traced here: 36.4 us
  waiting for transfers between devices  11.9 us (32%)
  starting transfers between devices  9.65 us (26%)
  blocking collectives  7.05 us (19%)
  Pallas kernels  5.98 us (16%)
  local copies, waits for them, and re-layouts  1.71 us (5%)
    all_to_all x1, waiting for transfers between devices, body(): lax.all_to_all(sent, 'dp', split_axis=0, concat_axis=0, tiled=True)  8.16 us
    all_to_all x1, blocking collectives, body(): lax.all_to_all(balanced.reshape(groups, slots), 'dp', split_axis=0, conca...  7.05 us
    all_to_all x1, starting transfers between devices, body(): lax.all_to_all(sent, 'dp', split_axis=0, concat_axis=0, tiled=True)  5.2 us
    ppermute x3, starting transfers between devices, body(): lax.ppermute(part, 'concept', [(i, i ^ step) for i in range(quarters)])  4.45 us
    ppermute x3, waiting for transfers between devices, body(): lax.ppermute(part, 'concept', [(i, i ^ step) for i in range(quarters)])  3.79 us
    pallas_call x1, Pallas kernels, body(): pl.pallas_call(functools.partial(slot_kernel, groups, slots, held), out_s...  2.71 us
    pallas_call x1, Pallas kernels, body(): pl.pallas_call(functools.partial(match_kernel, total, depth), out_shape=(...  1.93 us
    reshape x1, local copies, waits for them, and re-layouts, body(): turned = padded.reshape(blocks, BASE, depth).transpose(0, 2, 1)  1.7 us
  transfers between devices with their start and end apart: 4, of which 3 were waited for; matrix products, arithmetic and copies ran while one was open for 5% of the time, Pallas kernels for 0%

profile of v2, /device:TPU:0, one launch (start us, length us, event | category | flops | bytes accessed | tf_op | source)
XLA Modules:
  0.0 36.4 jit_solution(9587433983685913557)
XLA Ops:
  0.0 2.7 %slot.1 = (bf16[8,264,128]{2,1,0:T(8,128)(2,1)}, f32[8,512]{1,0:T(8,128)}, f32[1,512]{1,0:T(1,128)}) custom-call(s32[1,512]{1,0:T(1,128)} %bitcast.12, bf16[512,256]{1,0:T(8,128)(2,1)} %text_ref.1), custom_call_target="tpu_custom_call" | custom-call | tf_op jit(solution)/shard_map/slot/pallas_call | solution.py:154
  2.7 5.2 %all-to-all-start = ((bf16[8,264,128]{2,1,0:T(8,128)(2,1)}), bf16[8,264,128]{2,1,0:T(8,128)(2,1)S(1)}, u32[]{:S(2)}, u32[]{:S(2)}) async-start(bf16[8,264,128]{2,1,0:T(8,128)(2,1)} %get-tuple-element.10), calls=%async_computation | async-start | bytes 1081344 | tf_op jit(solution)/shard_map/all_to_all | solution.py:167
  7.9 1.7 %copy.5 = bf16[12,256,256]{1,2,0:T(8,128)(2,1)S(1)} copy(bf16[12,256,256]{2,1,0:T(8,128)(2,1)} %bitcast.11) | data formatting | bytes 3145728 | tf_op jit(solution)/shard_map/reshape | solution.py:172
  9.6 0.0 copy-start
  9.6 0.0 copy-start.1
  9.6 8.2 %all-to-all-done.arrived_ref = bf16[8,264,128]{2,1,0:T(8,128)(2,1)S(1)} async-done(((bf16[8,264,128]{2,1,0:T(8,128)(2,1)}), bf16[8,264,128]{2,1,0:T(8,128)(2,1)S(1)}, u32[]{:S(2)}, u32[]{:S(2)}) %all-to-all-start) | async-done | bytes 540704 | tf_op jit(solution)/shard_map/all_to_all | solution.py:167
  17.8 1.9 %match.1 = (f32[3,8,128]{2,1,0:T(8,128)S(1)}, f32[2,8,128]{2,1,0:T(8,128)S(1)}) custom-call(bf16[8,264,128]{2,1,0:T(8,128)(2,1)S(1)} %all-to-all-done.arrived_ref, bf16[12,256,256]{2,1,0:T(8,128)(2,1)S(1)} %bitcast.8), custom_call_target="tpu_custom_call" | custom-call | tf_op jit(solution)/shard_map/match/pallas_call | solution.py:174
  19.7 3.7 %collective-permute-start.2 = (f32[3,8,128]{2,1,0:T(8,128)S(1)}, f32[3,8,128]{2,1,0:T(8,128)S(1)}, u32[]{:S(2)}, u32[]{:S(2)}) collective-permute-start(f32[3,8,128]{2,1,0:T(8,128)S(1)} %get-tuple-element.11.refs_0_), channel_id=1, source_target_pairs={{0,3},{1,2},{2,1},{3,0},{4,7},{5,6},{6,5},{7,4},{8,11},{9,10},{10,... | collective-permute-start | bytes 36872 | tf_op jit(solution)/shard_map/ppermute | solution.py:188
  23.4 0.0 collective-permute-start.1
  23.4 0.8 %collective-permute-start = (f32[3,8,128]{2,1,0:T(8,128)S(1)}, f32[3,8,128]{2,1,0:T(8,128)S(1)}, u32[]{:S(2)}, u32[]{:S(2)}) collective-permute-start(f32[3,8,128]{2,1,0:T(8,128)S(1)} %get-tuple-element.11.refs_0_), channel_id=1, source_target_pairs={{0,1},{1,0},{2,3},{3,2},{4,5},{5,4},{6,7},{7,6},{8,9},{9,8},{10,11... | collective-permute-start | bytes 36872 | tf_op jit(solution)/shard_map/ppermute | solution.py:188
  24.2 1.1 %collective-permute-done.2.refs_3_ = f32[3,8,128]{2,1,0:T(8,128)S(1)} collective-permute-done((f32[3,8,128]{2,1,0:T(8,128)S(1)}, f32[3,8,128]{2,1,0:T(8,128)S(1)}, u32[]{:S(2)}, u32[]{:S(2)}) %collective-permute-start.2) | collective-permute-done | bytes 12320 | tf_op jit(solution)/shard_map/ppermute | solution.py:188
  25.3 2.7 %collective-permute-done.1.refs_2_ = f32[3,8,128]{2,1,0:T(8,128)S(1)} collective-permute-done((f32[3,8,128]{2,1,0:T(8,128)S(1)}, f32[3,8,128]{2,1,0:T(8,128)S(1)}, u32[]{:S(2)}, u32[]{:S(2)}) %collective-permute-start.1) | collective-permute-done | bytes 12320 | tf_op jit(solution)/shard_map/ppermute | solution.py:188
  28.0 0.0 collective-permute-done.refs_1_
  28.0 0.6 %count.1 = f32[8,128]{1,0:T(8,128)S(1)} custom-call(f32[3,8,128]{2,1,0:T(8,128)S(1)} %get-tuple-element.11.refs_0_, f32[3,8,128]{2,1,0:T(8,128)S(1)} %collective-permute-done.refs_1_, f32[3,8,128]{2,1,0:T(8,128)S(1)} %collective-permute-done.1.refs_2_, f32[3,8,128]{2,1,0:T(8,128)S(1)} %collective-permute-done.2.refs_3_, ...), custom_call_target="tpu_custom_call" | custom-call | tf_op jit(solution)/shard_map/count/pallas_call | solution.py:193
  28.6 7.1 %all_to_all.16 = f32[8,1,128]{2,1,0:T(1,128)S(1)} all-to-all(f32[8,1,128]{2,1,0:T(1,128)S(1)} %bitcast.10), channel_id=1, replica_groups=mesh['dp'=8,'concept'=4] {'dp'}, dimensions={0} | all-to-all | bytes 8192 | tf_op jit(solution)/shard_map/all_to_all | solution.py:202
  35.6 0.0 copy-done
  35.6 0.0 copy-done.1
  35.6 0.8 %unslot.1 = f32[1,512]{1,0:T(1,128)} custom-call(f32[8,128]{1,0:T(8,128)S(1)} %bitcast.9, f32[8,512]{1,0:T(8,128)S(1)} %copy-done, f32[1,512]{1,0:T(1,128)S(1)} %copy-done.1), custom_call_target="tpu_custom_call" | custom-call | tf_op jit(solution)/shard_map/unslot/pallas_call | solution.py:204
Async XLA Ops:
  2.7 15.1 %all-to-all-start = ((bf16[8,264,128]{2,1,0:T(8,128)(2,1)}), bf16[8,264,128]{2,1,0:T(8,128)(2,1)S(1)}, u32[]{:S(2)}, u32[]{:S(2)}) async-start(bf16[8,264,128]{2,1,0:T(8,128)(2,1)} %get-tuple-element.10), calls=%async_computation | async-start | bytes 1081344 | tf_op jit(solution)/shard_map/all_to_all | solution.py:167
  9.6 26.0 %copy-start = (f32[8,512]{1,0:T(8,128)S(1)}, f32[8,512]{1,0:T(8,128)}, u32[]{:S(2)}) copy-start(f32[8,512]{1,0:T(8,128)} %get-tuple-element.13.mark_ref) | copy-start | bytes 49156
  9.6 26.0 %copy-start.1 = (f32[1,512]{1,0:T(1,128)S(1)}, f32[1,512]{1,0:T(1,128)}, u32[]{:S(2)}) copy-start(f32[1,512]{1,0:T(1,128)} %get-tuple-element.14.rank_ref) | copy-start | bytes 6148
  19.7 5.6 %collective-permute-start.2 = (f32[3,8,128]{2,1,0:T(8,128)S(1)}, f32[3,8,128]{2,1,0:T(8,128)S(1)}, u32[]{:S(2)}, u32[]{:S(2)}) collective-permute-start(f32[3,8,128]{2,1,0:T(8,128)S(1)} %get-tuple-element.11.refs_0_), channel_id=1, source_target_pairs={{0,3},{1,2},{2,1},{3,0},{4,7},{5,6},{6,5},{7,4},{8,11},{9,10},{10,... | collective-permute-start | bytes 36872 | tf_op jit(solution)/shard_map/ppermute | solution.py:188
  23.4 4.6 %collective-permute-start.1 = (f32[3,8,128]{2,1,0:T(8,128)S(1)}, f32[3,8,128]{2,1,0:T(8,128)S(1)}, u32[]{:S(2)}, u32[]{:S(2)}) collective-permute-start(f32[3,8,128]{2,1,0:T(8,128)S(1)} %get-tuple-element.11.refs_0_), channel_id=1, source_target_pairs={{0,2},{1,3},{2,0},{3,1},{4,6},{5,7},{6,4},{7,5},{8,10},{9,11},{10,... | collective-permute-start | bytes 36872 | tf_op jit(solution)/shard_map/ppermute | solution.py:188
  23.4 4.6 %collective-permute-start = (f32[3,8,128]{2,1,0:T(8,128)S(1)}, f32[3,8,128]{2,1,0:T(8,128)S(1)}, u32[]{:S(2)}, u32[]{:S(2)}) collective-permute-start(f32[3,8,128]{2,1,0:T(8,128)S(1)} %get-tuple-element.11.refs_0_), channel_id=1, source_target_pairs={{0,1},{1,0},{2,3},{3,2},{4,5},{5,4},{6,7},{7,6},{8,9},{9,8},{10,11... | collective-permute-start | bytes 36872 | tf_op jit(solution)/shard_map/ppermute | solution.py:188
